TPU v7x, 32 devices: a whole 2x2x4 slice. The times are simulated.
32 devices in a mesh: view: 4 (over x, core), gauss: 8 (over z, y).
Axes of the slice: x: 2, y: 2, z: 4, core: 2. Of those that a mesh axis runs over, the one named last changes fastest.
Arguments:
- means: float32 [3, 131072], P(None, 'gauss'), may hold values from -1 to 1
- scales: float32 [3, 131072], P(None, 'gauss'), may hold values from 0.05 to 0.6
- quats: float32 [4, 131072], P(None, 'gauss'), may hold values from -6 to 6
- attrs: float32 [49, 131072], P(None, 'gauss'), may hold values from -6 to 6
- grad_screen: float32 [16, 2, 131072], P('view', None, 'gauss'), may hold values from -6 to 6
- visible: int32 [16, 131072], P('view', 'gauss'), may hold values 0 or 1
- clone_mask: int32 [131072], P('gauss'), may hold values from 0 to 1, as said below
- rotation: float32 [16, 3, 3], P('view'), may hold values from -3.5 to 3.5
- shift: float32 [16, 3], P('view'), may hold values from 2 to 5
- focal: float32 [16], P('view'), may hold values from 1 to 4
Outputs:
- peak_stats: float32 [2, 131072], P(None, 'gauss')
- clones: float32 [61, 131072], P(None, 'gauss')
- clone_total: int32 [], replicated
Inputs may be any that keep to these rules, and one draw needn't show every extreme that they name: `clone_mask`: in every draw some shard of 16384 consecutive Gaussians has all of them marked.
All inputs are finite; a program needn't handle non-finite values. No bound on the sum of `visible` on one device may be relied on, other than what follows from the above.
Results may differ from a plain program's by a relative error of at most 0.0003.
Values sent between devices are 32-bit elements; how exact they have to be, the bound alone decides.
A program may use at most 128 MiB of HBM per device.

v0:
```python
import jax
import jax.numpy as jnp
from jax import lax
from jax.sharding import PartitionSpec as P

G_DEV = 16384


def entering(value, axis, join, neutral):
    count, mine = (lax.axis_size(axis), lax.axis_index(axis))
    pieces = lax.all_gather(value, axis)
    running = jnp.full_like(value, 0) + jnp.asarray(neutral, value.dtype)

    def step(position, running):
        longer = join(running, pieces[position])
        return jnp.where(position < mine, longer, running)

    return lax.fori_loop(0, count - 1, step, running)


def quat_factor(scales, quats):
    inv = 1.0 / jnp.sqrt(jnp.sum(quats * quats, axis=0) + 0.25)
    w, x, y, z = (quats[0] * inv, quats[1] * inv, quats[2] * inv, quats[3] * inv)
    rq = [
        [1 - 2 * (y * y + z * z), 2 * (x * y - w * z), 2 * (x * z + w * y)],
        [2 * (x * y + w * z), 1 - 2 * (x * x + z * z), 2 * (y * z - w * x)],
        [2 * (x * z - w * y), 2 * (y * z + w * x), 1 - 2 * (x * x + y * y)],
    ]
    return [[rq[i][j] * scales[j] for j in range(3)] for i in range(3)]


def view_stats(means, factor, grad, seen, rot, trans, focal_v):
    point = [
        rot[i, 0] * means[0] + rot[i, 1] * means[1] + rot[i, 2] * means[2] + trans[i]
        for i in range(3)
    ]
    depth = jnp.maximum(point[2], 1.0)
    j00 = focal_v / depth
    j02 = -focal_v * point[0] / (depth * depth)
    j12 = -focal_v * point[1] / (depth * depth)
    first = [j00 * rot[0, j] + j02 * rot[2, j] for j in range(3)]
    second = [j00 * rot[1, j] + j12 * rot[2, j] for j in range(3)]
    prow = [sum((first[j] * factor[j][k] for j in range(3))) for k in range(3)]
    qrow = [sum((second[j] * factor[j][k] for j in range(3))) for k in range(3)]
    a_val = prow[0] ** 2 + prow[1] ** 2 + prow[2] ** 2 + 0.3
    c_val = qrow[0] ** 2 + qrow[1] ** 2 + qrow[2] ** 2 + 0.3
    b_val = prow[0] * qrow[0] + prow[1] * qrow[1] + prow[2] * qrow[2]
    half = 0.5 * (a_val - c_val)
    lam = 0.5 * (a_val + c_val) + jnp.sqrt(half * half + b_val * b_val + 0.01)
    seenf = seen.astype(jnp.float32)
    radius = 3.0 * jnp.sqrt(lam) * seenf
    gnorm = jnp.sqrt(grad[0] * grad[0] + grad[1] * grad[1]) * seenf
    return (gnorm, radius)


def add_ints(earlier, later):
    return earlier + later


def body(means, scales, quats, attrs, grad_screen, visible, clone_mask, rotation, shift, focal):
    factor = quat_factor(scales, quats)
    gmax = jnp.zeros(means.shape[1], jnp.float32)
    rmax = jnp.zeros(means.shape[1], jnp.float32)
    for v in range(grad_screen.shape[0]):
        gnorm, radius = view_stats(
            means, factor, grad_screen[v], visible[v], rotation[v], shift[v], focal[v]
        )
        gmax = jnp.maximum(gmax, gnorm)
        rmax = jnp.maximum(rmax, radius)
    gmax, rmax = lax.pmax((gmax, rmax), "view")
    peak = jnp.stack([gmax, rmax])
    rows = jnp.concatenate([means, scales, quats, attrs, peak], axis=0)
    feat_rows = rows.shape[0]
    shards = lax.axis_size("gauss")
    cap_blk = G_DEV // 128
    count = jnp.sum(clone_mask)
    blocks = (count + 127) // 128
    offset = entering(blocks, "gauss", add_ints, jnp.int32(0))
    summed = lax.psum(count.astype(jnp.float32), "gauss")
    total = summed.astype(jnp.int32)
    rank = jnp.cumsum(clone_mask) - 1
    where_to = jnp.where(clone_mask == 1, rank, cap_blk * 128)
    packed = (
        jnp.zeros((feat_rows, cap_blk * 128), jnp.float32).at[:, where_to].set(rows, mode="drop")
    )
    packed = packed.reshape(feat_rows, cap_blk, 128)
    per = (cap_blk + shards - 1) // shards
    target = jnp.arange(shards, dtype=jnp.int32)[:, None]
    within = jnp.arange(per, dtype=jnp.int32)[None, :]
    local_blk = (target - offset) % shards + within * shards
    valid = local_blk < blocks
    picked = jnp.minimum(local_blk, cap_blk - 1).reshape(-1)
    outgoing = packed[:, picked, :] * valid.reshape(1, -1, 1).astype(jnp.float32)
    outgoing = outgoing.reshape(feat_rows, shards, per, 128)
    slot_ids = (
        jnp.where(valid, (offset + local_blk) // shards, cap_blk)
        .astype(jnp.int32)
        .reshape(1, shards, per)
    )
    width = 128 // lax.axis_size("view")
    start = lax.axis_index("view") * width
    portion = lax.dynamic_slice_in_dim(outgoing, start, width, 3)
    arrived, slots_in = (
        lax.all_to_all(portion, "gauss", split_axis=1, concat_axis=1, tiled=True),
        lax.all_to_all(slot_ids, "gauss", split_axis=1, concat_axis=1, tiled=True),
    )
    arrived = arrived.reshape(feat_rows, shards * per, width)
    partial_place = (
        jnp.zeros((feat_rows, cap_blk, width), jnp.float32)
        .at[:, slots_in.reshape(-1)]
        .set(arrived, mode="drop")
    )
    placed = lax.all_gather(partial_place, "view", axis=2, tiled=True)
    clones = placed.reshape(feat_rows, cap_blk * 128)
    return (peak, clones, total)


def solution(mesh):
    return jax.shard_map(
        body,
        mesh=mesh,
        in_specs=(
            P(None, "gauss"),
            P(None, "gauss"),
            P(None, "gauss"),
            P(None, "gauss"),
            P("view", None, "gauss"),
            P("view", "gauss"),
            P("gauss"),
            P("view", None, None),
            P("view", None),
            P("view"),
        ),
        out_specs=(P(None, "gauss"), P(None, "gauss"), P()),
        check_vma=False,
    )
```

profile of v0, /device:TPU:0, one launch (start us, length us, event | category | flops | bytes accessed | tf_op | source)
XLA Modules:
  0.0 360.1 jit_solution(10346555730215635345)
XLA Ops:
  13.1 13.1 %all-reduce = s32[8]{0:T(128)S(1)} all-reduce(s32[8]{0:T(128)S(1)} %dynamic-update-slice), channel_id=1, replica_groups=mesh['view'=4,'gauss'=8] {'gauss'}, use_global_device_ids=true, to_apply=%add | all-reduce | flops 8 | bytes 64
  26.2 8.9 %while.13 = (s32[]{:T(128)}, s32[]{:T(128)}, s32[]{:T(128)}, s32[8]{0:T(128)S(1)}, s32[]{:T(128)}) while((s32[]{:T(128)}, s32[]{:T(128)}, s32[]{:T(128)}, s32[8]{0:T(128)S(1)}, s32[]{:T(128)}) %tuple.130), condition=%wide.region_5.6_spmd, body=%wide.region_4.5_spmd.sunk | while | flops 5 | bytes 107 | solution.py:18
  35.8 3.3 all-to-all-start
  47.5 7.4 %multiply_add_fusion.23 = (f32[1,16384]{1,0:T(1,128)S(1)}, f32[1,16384]{1,0:T(1,128)S(1)}, f32[1,16384]{1,0:T(1,128)S(1)}, f32[1,16384]{1,0:T(1,128)S(1)}) fusion(f32[]{:T(128)} %bitcast.15, f32[]{:T(128)} %bitcast.11, f32[]{:T(128)} %bitcast.18, f32[3,16384]{1,0:T(4,128)} %param.12, f32[]{:T(128)} %bitcast.17, f32[]{:T(128)} %bitcast.16, f32[]{:T(128)S(6)} %neg.16, ...), kind=kLoop, calls=%fused_computation.34 | loop fusion | flops 327680 | bytes 458792 | tf_op jit(solution)/shard_map/add | solution.py:41
  54.9 7.5 %multiply_add_fusion.22 = (f32[1,16384]{1,0:T(1,128)S(1)}, f32[1,16384]{1,0:T(1,128)S(1)}, f32[1,16384]{1,0:T(1,128)S(1)}, f32[1,16384]{1,0:T(1,128)S(1)}) fusion(f32[1,16384]{1,0:T(1,128)S(1)} %get-tuple-element.103, f32[1,16384]{1,0:T(1,128)S(1)} %get-tuple-element.104, f32[]{:T(128)} %bitcast.16, f32[]{:T(128)} %bitcast.12, f32[]{:T(128)} %bitcast.13, ...), kind=kLoop, calls=%fused_computation.33 | loop fusion | flops 294912 | bytes 655400 | tf_op jit(solution)/shard_map/add | solution.py:41
  66.4 7.5 %multiply_add_fusion.17 = (f32[1,16384]{1,0:T(1,128)S(1)}, f32[1,16384]{1,0:T(1,128)S(1)}, f32[1,16384]{1,0:T(1,128)S(1)}, f32[1,16384]{1,0:T(1,128)S(1)}) fusion(f32[]{:T(128)} %bitcast.41, f32[]{:T(128)} %bitcast.37, f32[]{:T(128)} %bitcast.44, f32[3,16384]{1,0:T(4,128)} %param.12, f32[]{:T(128)} %bitcast.43, f32[]{:T(128)} %bitcast.42, f32[]{:T(128)S(6)} %neg.17, ...), kind=kLoop, calls=%fused_computation.28 | loop fusion | flops 327680 | bytes 458792 | tf_op jit(solution)/shard_map/add | solution.py:41
  73.8 6.1 %multiply_add_fusion.16 = (f32[1,16384]{1,0:T(1,128)S(1)}, f32[1,16384]{1,0:T(1,128)S(1)}, f32[1,16384]{1,0:T(1,128)S(1)}, f32[1,16384]{1,0:T(1,128)S(1)}) fusion(f32[1,16384]{1,0:T(1,128)S(1)} %get-tuple-element.109, f32[1,16384]{1,0:T(1,128)S(1)} %get-tuple-element.110, f32[]{:T(128)} %bitcast.42, f32[]{:T(128)} %bitcast.38, f32[]{:T(128)} %bitcast.39, ...), kind=kLoop, calls=%fused_computation.27 | loop fusion | flops 294912 | bytes 655400 | tf_op jit(solution)/shard_map/add | solution.py:41
  84.1 6.3 %multiply_add_fusion.11 = (f32[1,16384]{1,0:T(1,128)S(1)}, f32[1,16384]{1,0:T(1,128)S(1)}, f32[1,16384]{1,0:T(1,128)S(1)}, f32[1,16384]{1,0:T(1,128)S(1)}) fusion(f32[]{:T(128)} %bitcast.60, f32[]{:T(128)} %bitcast.56, f32[]{:T(128)} %bitcast.63, f32[3,16384]{1,0:T(4,128)S(1)} %copy-done.1, f32[]{:T(128)} %bitcast.62, f32[]{:T(128)} %bitcast.61, ...), kind=kLoop, calls=%fused_computation.22 | loop fusion | flops 327680 | bytes 458792 | tf_op jit(solution)/shard_map/add | solution.py:41
  90.4 6.1 %multiply_add_fusion.10 = (f32[1,16384]{1,0:T(1,128)S(1)}, f32[1,16384]{1,0:T(1,128)S(1)}, f32[1,16384]{1,0:T(1,128)S(1)}, f32[1,16384]{1,0:T(1,128)S(1)}) fusion(f32[1,16384]{1,0:T(1,128)S(1)} %get-tuple-element.115, f32[1,16384]{1,0:T(1,128)S(1)} %get-tuple-element.116, f32[]{:T(128)} %bitcast.61, f32[]{:T(128)} %bitcast.57, f32[]{:T(128)} %bitcast.58, ...), kind=kLoop, calls=%fused_computation.21 | loop fusion | flops 294912 | bytes 655400 | tf_op jit(solution)/shard_map/add | solution.py:41
  100.3 6.1 %multiply_add_fusion.5 = (f32[1,16384]{1,0:T(1,128)S(1)}, f32[1,16384]{1,0:T(1,128)S(1)}, f32[1,16384]{1,0:T(1,128)S(1)}, f32[1,16384]{1,0:T(1,128)S(1)}) fusion(f32[]{:T(128)} %bitcast.79, f32[]{:T(128)} %bitcast.75, f32[]{:T(128)} %bitcast.82, f32[3,16384]{1,0:T(4,128)S(1)} %copy-done.1, f32[]{:T(128)} %bitcast.81, f32[]{:T(128)} %bitcast.80, f32[]{:T(128)S(6)} %neg.19, ...), kind=kLoop, calls=%fused_computation.16 | loop fusion | flops 327680 | bytes 458792 | tf_op jit(solution)/shard_map/add | solution.py:41
  106.3 6.2 %multiply_add_fusion.4 = (f32[1,16384]{1,0:T(1,128)S(1)}, f32[1,16384]{1,0:T(1,128)S(1)}, f32[1,16384]{1,0:T(1,128)S(1)}, f32[1,16384]{1,0:T(1,128)S(1)}) fusion(f32[1,16384]{1,0:T(1,128)S(1)} %get-tuple-element.121, f32[1,16384]{1,0:T(1,128)S(1)} %get-tuple-element.122, f32[]{:T(128)} %bitcast.80, f32[]{:T(128)} %bitcast.76, f32[]{:T(128)} %bitcast.77, ...), kind=kLoop, calls=%fused_computation.15 | loop fusion | flops 294912 | bytes 655400 | tf_op jit(solution)/shard_map/add | solution.py:41
  118.6 33.1 %all-reduce.4.cloned.1.call-done = (f32[1,16384]{1,0:T(1,128)}, f32[1,16384]{1,0:T(1,128)}) async-done(((f32[1,16384]{1,0:T(1,128)}, f32[1,16384]{1,0:T(1,128)}), (f32[1,16384]{1,0:T(1,128)}, f32[1,16384]{1,0:T(1,128)})) %all-reduce.4.cloned.1.call-update) | async-done | bytes 131088 | tf_op jit(solution)/shard_map/pmax | solution.py:70
  151.7 21.6 %concatenate.4 = f32[61,16384]{1,0:T(8,128)} concatenate(f32[3,16384]{1,0:T(4,128)S(1)} %copy-done.1, f32[3,16384]{1,0:T(4,128)S(1)} %copy-done.3, f32[4,16384]{1,0:T(4,128)S(1)} %copy-done.2, f32[49,16384]{1,0:T(8,128)} %param.15, f32[1,16384]{1,0:T(1,128)} %get-tuple-element.101, f32[1,16384]{1,0:T(1,128)} %get-tuple-element.100), dimensions={0} | concatenate | bytes 7995392 | tf_op jit(solution)/shard_map/concatenate | solution.py:72
  173.2 6.9 %copy.24 = f32[16384,61]{1,0:T(8,128)} copy(f32[16384,61]{0,1:T(8,128)} %bitcast.130) | data formatting | bytes 7995392 | tf_op jit(solution)/shard_map/concatenate | solution.py:72
  180.1 44.4 %scatter_custom_fusion = f32[61,16384]{0,1:T(8,128)} fusion(s32[16384]{0:T(1024)S(1)} %get-tuple-element.157, f32[16384,61]{1,0:T(8,128)} %copy.24, f32[]{:T(128)} %constant.86.clone.1), kind=kCustom, calls=%fused_computation.3 | custom fusion | bytes 3998208 | tf_op jit(solution)/shard_map/scatter | solution.py:84
  224.5 7.7 %gather_fusion = f32[128,61,128]{1,2,0:T(8,128)} fusion(f32[61,128,128]{0,2,1:T(8,128)} %bitcast.128, s32[1024]{0:T(1024)S(1)} %pad_clamp_fusion), kind=kCustom, calls=%fused_computation | custom fusion | bytes 7995904 | tf_op jit(solution)/shard_map/gather | solution.py:93
  234.0 3.9 %reshape.632 = f32[8,1,31232]{2,1,0:T(1,128)} reshape(f32[8,16,32,61]{3,2,1,0:T(8,128)S(1)} %fusion.15) | data formatting | bytes 1998848
  237.9 5.5 %all-to-all-start.1 = ((f32[8,1,31232]{2,1,0:T(1,128)}), f32[8,1,31232]{2,1,0:T(1,128)S(1)}, u32[]{:S(2)}, u32[]{:S(2)}) async-start(f32[8,1,31232]{2,1,0:T(1,128)} %reshape.632), calls=%async_computation.1 | async-start | bytes 1998848 | tf_op jit(solution)/shard_map/all_to_all | solution.py:104
  244.8 22.6 %all-to-all-done.1 = f32[8,1,31232]{2,1,0:T(1,128)S(1)} async-done(((f32[8,1,31232]{2,1,0:T(1,128)}), f32[8,1,31232]{2,1,0:T(1,128)S(1)}, u32[]{:S(2)}, u32[]{:S(2)}) %all-to-all-start.1) | async-done | bytes 999456 | tf_op jit(solution)/shard_map/all_to_all | solution.py:104
  270.9 4.3 %reshape.633 = f32[8,16,32,61]{3,2,1,0:T(8,128)} reshape(f32[8,31232]{1,0:T(8,128)S(1)} %reduce.6) | data formatting | bytes 1998848
  275.5 12.0 %scatter_fusion = f32[61,128,32]{0,2,1:T(8,128)S(1)} fusion(f32[61,128,32]{0,2,1:T(8,128)S(1)} %broadcast_in_dim.21, s32[128]{0:T(128)S(1)} %fusion.4, f32[128,61,32]{1,2,0:T(8,128)} %bitcast.129), kind=kCustom, calls=%fused_computation.2 | custom fusion | bytes 2998784 | tf_op jit(solution)/shard_map/scatter | solution.py:111
  289.4 19.8 %psum.7 = f32[]{:T(128)} all-reduce(f32[]{:T(128)S(6)} %convert_element_type.47), channel_id=1, replica_groups=mesh['view'=4,'gauss'=8] {'gauss'}, use_global_device_ids=true, to_apply=%region_10.11 | all-reduce | flops 1 | bytes 8 | tf_op jit(solution)/shard_map/psum | solution.py:79
  310.7 34.7 %all-gather.2.cloned.1.call-done = f32[61,128,128]{0,2,1:T(8,128)} async-done(((f32[61,128,32]{0,2,1:T(8,128)}), f32[61,128,128]{0,2,1:T(8,128)}) %all-gather.2.cloned.1.call-update) | async-done | bytes 3997712 | tf_op jit(solution)/shard_map/all_gather | solution.py:113
  345.3 6.8 %copy.25 = f32[61,16384]{1,0:T(8,128)} copy(f32[61,16384]{0,1:T(8,128)} %bitcast.131) | data formatting | bytes 7995392
  (77 shorter events, 43.1 us)
Async XLA Ops:
  7.2 66.7 %copy-start.1 = (f32[3,16384]{1,0:T(4,128)S(1)}, f32[3,16384]{1,0:T(4,128)}, u32[]{:S(2)}) copy-start(f32[3,16384]{1,0:T(4,128)} %param.12) | copy-start | bytes 589828
  7.2 107.9 %copy-start.7 = (s32[4,16384]{1,0:T(4,128)S(1)}, s32[4,16384]{1,0:T(4,128)}, u32[]{:S(2)}) copy-start(s32[4,16384]{1,0:T(4,128)} %param.17) | copy-start | bytes 786436
  8.2 107.1 %copy-start.3 = (f32[3,16384]{1,0:T(4,128)S(1)}, f32[3,16384]{1,0:T(4,128)}, u32[]{:S(2)}) copy-start(f32[3,16384]{1,0:T(4,128)} %param.13) | copy-start | bytes 589828
  8.8 106.7 %copy-start.4 = (f32[4,2,16384]{2,1,0:T(2,128)S(1)}, f32[4,2,16384]{2,1,0:T(2,128)}, u32[]{:S(2)}) copy-start(f32[4,2,16384]{2,1,0:T(2,128)} %param.16) | copy-start | bytes 1572868
  35.8 202.1 %all-to-all-start = ((s32[1,8,16]{2,0,1:T(1,128)}), s32[1,8,16]{2,0,1:T(1,128)S(1)}, u32[]{:S(2)}, u32[]{:S(2)}) async-start(s32[1,8,16]{2,0,1:T(1,128)} %compare_select_fusion.1), calls=%async_computation | async-start | bytes 8192 | tf_op jit(solution)/shard_map/all_to_all | solution.py:105
  39.1 112.5 %all-reduce.4.cloned.1.call-start = ((), (), s32[]{:S(2)}) async-start(), calls=%async_computation.3 | async-start | bytes 262144 | tf_op jit(solution)/shard_map/pmax | solution.py:70
  79.9 71.7 %copy-start.2 = (f32[4,16384]{1,0:T(4,128)S(1)}, f32[4,16384]{1,0:T(4,128)}, u32[]{:S(2)}) copy-start(f32[4,16384]{1,0:T(4,128)} %param.14) | copy-start | bytes 786436
  237.9 29.4 %all-to-all-start.1 = ((f32[8,1,31232]{2,1,0:T(1,128)}), f32[8,1,31232]{2,1,0:T(1,128)S(1)}, u32[]{:S(2)}, u32[]{:S(2)}) async-start(f32[8,1,31232]{2,1,0:T(1,128)} %reshape.632), calls=%async_computation.1 | async-start | bytes 1998848 | tf_op jit(solution)/shard_map/all_to_all | solution.py:104
  243.5 101.9 %all-gather.2.cloned.1.call-start = ((), (), s32[]{:S(2)}) async-start(), calls=%async_computation.2 | async-start | bytes 10485760 | tf_op jit(solution)/shard_map/all_gather | solution.py:113
  275.4 34.4 %copy-start.5 = (f32[1,16384]{1,0:T(1,128)S(1)}, f32[1,16384]{1,0:T(1,128)}, u32[]{:S(2)}) copy-start(f32[1,16384]{1,0:T(1,128)} %get-tuple-element.100) | copy-start | bytes 196612
  275.4 34.4 %copy-start.6 = (f32[1,16384]{1,0:T(1,128)S(1)}, f32[1,16384]{1,0:T(1,128)}, u32[]{:S(2)}) copy-start(f32[1,16384]{1,0:T(1,128)} %get-tuple-element.101) | copy-start | bytes 196612
  287.5 1.3 copy-start
Sparse Core Ops, SparseCore 0:
  118.4 33.1 all-reduce.3
  288.9 56.3 all-gather.1
where the time goes:
time: 363 us; the launch traced here: 360 us
  local copies, waits for them, and re-layouts  127 us (35%)
  waiting for transfers between devices  90.4 us (25%)
  other arithmetic  76.7 us (21%)
  blocking collectives  32.9 us (9%)
  between operations  19.9 us (5%)
  starting transfers between devices  8.9 us (2%)
  loops' own time  4.58 us (1%)
    add x8, other arithmetic, view_stats(): first = [j00 * rot[0, j] + j02 * rot[2, j] for j in range(3)]  53 us
    scatter x1, local copies, waits for them, and re-layouts, body(): jnp.zeros((feat_rows, cap_blk * 128), jnp.float32).at[:, where_to]  44.4 us
    all_gather x1, waiting for transfers between devices, body(): placed = lax.all_gather(partial_place, 'view', axis=2, tiled=True)  34.7 us
    pmax x1, waiting for transfers between devices, body(): gmax, rmax = lax.pmax((gmax, rmax), 'view')  33.1 us
    concatenate x2, local copies, waits for them, and re-layouts, body(): rows = jnp.concatenate([means, scales, quats, attrs, peak], axis=0)  28.5 us
    all_to_all x1, waiting for transfers between devices, body(): lax.all_to_all(portion, 'gauss', split_axis=1, concat_axis=1, tiled=True)  22.6 us
    psum x1, blocking collectives, body(): summed = lax.psum(count.astype(jnp.float32), 'gauss')  19.8 us
    unnamed x24, local copies, waits for them, and re-layouts  18.4 us
  transfers between devices with their start and end apart: 4, of which 3 were waited for; matrix products, arithmetic and copies ran while one was open for 46% of the time, Pallas kernels for 0%

commit v1 on v0

--- a/solution.py
+++ b/solution.py
@@ -110,7 +110,8 @@
         .at[:, slots_in.reshape(-1)]
         .set(arrived, mode="drop")
     )
-    placed = lax.all_gather(partial_place, "view", axis=2, tiled=True)
+    shards_2 = lax.all_gather(partial_place, "view")
+    placed = jnp.concatenate(shards_2, axis=2)
     clones = placed.reshape(feat_rows, cap_blk * 128)
     return (peak, clones, total)
 

time: 363 us -> 348 us (0.959)
  waiting for transfers between devices: 90.4 us -> 65.4 us
  local copies, waits for them, and re-layouts: 127 us -> 137 us
    all_gather x1, waiting for transfers between devices: 34.7 us -> 9.74 us  [body(): shards_2 = lax.all_gather(partial_place, 'view')]
    reshape x1 -> x2, local copies, waits for them, and re-layouts: 0.98 us -> 10.3 us  [the longest x1 9.28 us: body(): placed = jnp.concatenate(shards_2, axis=2)]
    scatter x1 -> x2, local copies, waits for them, and re-layouts: 12 us -> 14.6 us  [body(): partial_place = jnp.zeros((feat_rows, cap_blk, width), jnp.float32).at[:,...]
    unnamed x24 -> x22, local copies, waits for them, and re-layouts: 18.4 us -> 17.1 us
  transfers between devices with their start and end apart: 4 -> 4, of which waited for: 3 -> 3; matrix products, arithmetic and copies ran while one was open for 46% -> 48% of each run, Pallas kernels for 0% -> 0%
where the time goes in v1:
time: 348 us; the launch traced here: 345 us
  local copies, waits for them, and re-layouts  137 us (39%)
  other arithmetic  76.8 us (22%)
  waiting for transfers between devices  65.4 us (19%)
  blocking collectives  32.9 us (9%)
  between operations  20 us (6%)
  starting transfers between devices  8.92 us (3%)
  loops' own time  4.1 us (1%)
    add x8, other arithmetic, view_stats(): first = [j00 * rot[0, j] + j02 * rot[2, j] for j in range(3)]  52.7 us
    scatter x1, local copies, waits for them, and re-layouts, body(): jnp.zeros((feat_rows, cap_blk * 128), jnp.float32).at[:, where_to]  44.3 us
    pmax x1, waiting for transfers between devices, body(): gmax, rmax = lax.pmax((gmax, rmax), 'view')  33.1 us
    concatenate x2, local copies, waits for them, and re-layouts, body(): rows = jnp.concatenate([means, scales, quats, attrs, peak], axis=0)  28.5 us
    all_to_all x1, waiting for transfers between devices, body(): lax.all_to_all(portion, 'gauss', split_axis=1, concat_axis=1, tiled=True)  22.6 us
    psum x1, blocking collectives, body(): summed = lax.psum(count.astype(jnp.float32), 'gauss')  19.8 us
    unnamed x22, local copies, waits for them, and re-layouts  17.1 us
    scatter x2, local copies, waits for them, and re-layouts, body(): partial_place = jnp.zeros((feat_rows, cap_blk, width), jnp.float32).at[:,...  14.6 us
  transfers between devices with their start and end apart: 4, of which 3 were waited for; matrix products, arithmetic and copies ran while one was open for 48% of the time, Pallas kernels for 0%

profile of v1, /device:TPU:0, one launch (start us, length us, event | category | flops | bytes accessed | tf_op | source)
XLA Modules:
  0.0 345.2 jit_solution(12069117192737252019)
XLA Ops:
  13.2 13.1 %all-reduce = s32[8]{0:T(128)S(1)} all-reduce(s32[8]{0:T(128)S(1)} %dynamic-update-slice), channel_id=1, replica_groups=mesh['view'=4,'gauss'=8] {'gauss'}, use_global_device_ids=true, to_apply=%add | all-reduce | flops 8 | bytes 64
  26.2 8.2 %while.13 = (s32[]{:T(128)}, s32[]{:T(128)}, s32[]{:T(128)}, s32[8]{0:T(128)S(1)}, s32[]{:T(128)}) while((s32[]{:T(128)}, s32[]{:T(128)}, s32[]{:T(128)}, s32[8]{0:T(128)S(1)}, s32[]{:T(128)}) %tuple.129), condition=%wide.region_5.6_spmd, body=%wide.region_4.5_spmd.sunk | while | flops 5 | bytes 107 | solution.py:18
  46.9 7.4 %multiply_add_fusion.23 = (f32[1,16384]{1,0:T(1,128)S(1)}, f32[1,16384]{1,0:T(1,128)S(1)}, f32[1,16384]{1,0:T(1,128)S(1)}, f32[1,16384]{1,0:T(1,128)S(1)}) fusion(f32[]{:T(128)} %bitcast.15, f32[]{:T(128)} %bitcast.11, f32[]{:T(128)} %bitcast.18, f32[3,16384]{1,0:T(4,128)} %param.12, f32[]{:T(128)} %bitcast.17, f32[]{:T(128)} %bitcast.16, f32[]{:T(128)S(6)} %neg.16, ...), kind=kLoop, calls=%fused_computation.34 | loop fusion | flops 327680 | bytes 458792 | tf_op jit(solution)/shard_map/add | solution.py:41
  54.3 7.4 %multiply_add_fusion.22 = (f32[1,16384]{1,0:T(1,128)S(1)}, f32[1,16384]{1,0:T(1,128)S(1)}, f32[1,16384]{1,0:T(1,128)S(1)}, f32[1,16384]{1,0:T(1,128)S(1)}) fusion(f32[1,16384]{1,0:T(1,128)S(1)} %get-tuple-element.100, f32[1,16384]{1,0:T(1,128)S(1)} %get-tuple-element.101, f32[]{:T(128)} %bitcast.16, f32[]{:T(128)} %bitcast.12, f32[]{:T(128)} %bitcast.13, ...), kind=kLoop, calls=%fused_computation.33 | loop fusion | flops 294912 | bytes 655400 | tf_op jit(solution)/shard_map/add | solution.py:41
  65.7 7.4 %multiply_add_fusion.17 = (f32[1,16384]{1,0:T(1,128)S(1)}, f32[1,16384]{1,0:T(1,128)S(1)}, f32[1,16384]{1,0:T(1,128)S(1)}, f32[1,16384]{1,0:T(1,128)S(1)}) fusion(f32[]{:T(128)} %bitcast.41, f32[]{:T(128)} %bitcast.37, f32[]{:T(128)} %bitcast.44, f32[3,16384]{1,0:T(4,128)} %param.12, f32[]{:T(128)} %bitcast.43, f32[]{:T(128)} %bitcast.42, f32[]{:T(128)S(6)} %neg.17, ...), kind=kLoop, calls=%fused_computation.28 | loop fusion | flops 327680 | bytes 458792 | tf_op jit(solution)/shard_map/add | solution.py:41
  73.1 6.2 %multiply_add_fusion.16 = (f32[1,16384]{1,0:T(1,128)S(1)}, f32[1,16384]{1,0:T(1,128)S(1)}, f32[1,16384]{1,0:T(1,128)S(1)}, f32[1,16384]{1,0:T(1,128)S(1)}) fusion(f32[1,16384]{1,0:T(1,128)S(1)} %get-tuple-element.106, f32[1,16384]{1,0:T(1,128)S(1)} %get-tuple-element.107, f32[]{:T(128)} %bitcast.42, f32[]{:T(128)} %bitcast.38, f32[]{:T(128)} %bitcast.39, ...), kind=kLoop, calls=%fused_computation.27 | loop fusion | flops 294912 | bytes 655400 | tf_op jit(solution)/shard_map/add | solution.py:41
  83.5 6.1 %multiply_add_fusion.11 = (f32[1,16384]{1,0:T(1,128)S(1)}, f32[1,16384]{1,0:T(1,128)S(1)}, f32[1,16384]{1,0:T(1,128)S(1)}, f32[1,16384]{1,0:T(1,128)S(1)}) fusion(f32[]{:T(128)} %bitcast.60, f32[]{:T(128)} %bitcast.56, f32[]{:T(128)} %bitcast.63, f32[3,16384]{1,0:T(4,128)S(1)} %copy-done, f32[]{:T(128)} %bitcast.62, f32[]{:T(128)} %bitcast.61, f32[]{:T(128)S(6)} %neg.18, ...), kind=kLoop, calls=%fused_computation.22 | loop fusion | flops 327680 | bytes 458792 | tf_op jit(solution)/shard_map/add | solution.py:41
  89.6 6.1 %multiply_add_fusion.10 = (f32[1,16384]{1,0:T(1,128)S(1)}, f32[1,16384]{1,0:T(1,128)S(1)}, f32[1,16384]{1,0:T(1,128)S(1)}, f32[1,16384]{1,0:T(1,128)S(1)}) fusion(f32[1,16384]{1,0:T(1,128)S(1)} %get-tuple-element.112, f32[1,16384]{1,0:T(1,128)S(1)} %get-tuple-element.113, f32[]{:T(128)} %bitcast.61, f32[]{:T(128)} %bitcast.57, f32[]{:T(128)} %bitcast.58, ...), kind=kLoop, calls=%fused_computation.21 | loop fusion | flops 294912 | bytes 655400 | tf_op jit(solution)/shard_map/add | solution.py:41
  99.8 6.1 %multiply_add_fusion.5 = (f32[1,16384]{1,0:T(1,128)S(1)}, f32[1,16384]{1,0:T(1,128)S(1)}, f32[1,16384]{1,0:T(1,128)S(1)}, f32[1,16384]{1,0:T(1,128)S(1)}) fusion(f32[]{:T(128)} %bitcast.79, f32[]{:T(128)} %bitcast.75, f32[]{:T(128)} %bitcast.82, f32[3,16384]{1,0:T(4,128)S(1)} %copy-done, f32[]{:T(128)} %bitcast.81, f32[]{:T(128)} %bitcast.80, f32[]{:T(128)S(6)} %neg.19, ...), kind=kLoop, calls=%fused_computation.16 | loop fusion | flops 327680 | bytes 458792 | tf_op jit(solution)/shard_map/add | solution.py:41
  105.9 6.0 %multiply_add_fusion.4 = (f32[1,16384]{1,0:T(1,128)S(1)}, f32[1,16384]{1,0:T(1,128)S(1)}, f32[1,16384]{1,0:T(1,128)S(1)}, f32[1,16384]{1,0:T(1,128)S(1)}) fusion(f32[1,16384]{1,0:T(1,128)S(1)} %get-tuple-element.118, f32[1,16384]{1,0:T(1,128)S(1)} %get-tuple-element.119, f32[]{:T(128)} %bitcast.80, f32[]{:T(128)} %bitcast.76, f32[]{:T(128)} %bitcast.77, ...), kind=kLoop, calls=%fused_computation.15 | loop fusion | flops 294912 | bytes 655400 | tf_op jit(solution)/shard_map/add | solution.py:41
  118.0 33.1 %all-reduce.4.cloned.1.call-done = (f32[1,16384]{1,0:T(1,128)}, f32[1,16384]{1,0:T(1,128)}) async-done(((f32[1,16384]{1,0:T(1,128)}, f32[1,16384]{1,0:T(1,128)}), (f32[1,16384]{1,0:T(1,128)}, f32[1,16384]{1,0:T(1,128)})) %all-reduce.4.cloned.1.call-update) | async-done | bytes 131088 | tf_op jit(solution)/shard_map/pmax | solution.py:70
  151.1 21.6 %concatenate.4 = f32[61,16384]{1,0:T(8,128)} concatenate(f32[3,16384]{1,0:T(4,128)S(1)} %copy-done, f32[3,16384]{1,0:T(4,128)S(1)} %copy-done.2, f32[4,16384]{1,0:T(4,128)S(1)} %copy-done.1, f32[49,16384]{1,0:T(8,128)} %param.15, f32[1,16384]{1,0:T(1,128)} %get-tuple-element.98, f32[1,16384]{1,0:T(1,128)} %get-tuple-element.97), dimensions={0} | concatenate | bytes 7995392 | tf_op jit(solution)/shard_map/concatenate | solution.py:72
  172.7 6.9 %copy.26 = f32[16384,61]{1,0:T(8,128)} copy(f32[16384,61]{0,1:T(8,128)} %bitcast.134) | data formatting | bytes 7995392 | tf_op jit(solution)/shard_map/concatenate | solution.py:72
  179.6 44.3 %scatter_custom_fusion = f32[61,16384]{0,1:T(8,128)} fusion(s32[16384]{0:T(1024)S(1)} %get-tuple-element.154, f32[16384,61]{1,0:T(8,128)} %copy.26, f32[]{:T(128)} %constant.86.clone.1), kind=kCustom, calls=%fused_computation.3 | custom fusion | bytes 3998208 | tf_op jit(solution)/shard_map/scatter | solution.py:84
  223.9 7.7 %gather_fusion = f32[128,61,128]{1,2,0:T(8,128)} fusion(f32[61,128,128]{0,2,1:T(8,128)} %bitcast.132, s32[1024]{0:T(1024)S(1)} %pad_clamp_fusion), kind=kCustom, calls=%fused_computation | custom fusion | bytes 7995904 | tf_op jit(solution)/shard_map/gather | solution.py:93
  233.4 3.9 %reshape.633 = f32[8,1,31232]{2,1,0:T(1,128)} reshape(f32[8,16,32,61]{3,2,1,0:T(8,128)S(1)} %fusion.15) | data formatting | bytes 1998848
  237.4 5.5 %all-to-all-start.1 = ((f32[8,1,31232]{2,1,0:T(1,128)}), f32[8,1,31232]{2,1,0:T(1,128)S(1)}, u32[]{:S(2)}, u32[]{:S(2)}) async-start(f32[8,1,31232]{2,1,0:T(1,128)} %reshape.633), calls=%async_computation.1 | async-start | bytes 1998848 | tf_op jit(solution)/shard_map/all_to_all | solution.py:104
  244.2 22.6 %all-to-all-done.1 = f32[8,1,31232]{2,1,0:T(1,128)S(1)} async-done(((f32[8,1,31232]{2,1,0:T(1,128)}), f32[8,1,31232]{2,1,0:T(1,128)S(1)}, u32[]{:S(2)}, u32[]{:S(2)}) %all-to-all-start.1) | async-done | bytes 999456 | tf_op jit(solution)/shard_map/all_to_all | solution.py:104
  270.3 4.3 %reshape.634 = f32[8,16,32,61]{3,2,1,0:T(8,128)} reshape(f32[8,31232]{1,0:T(8,128)S(1)} %reduce.6) | data formatting | bytes 1998848
  274.9 12.0 %scatter_fusion = f32[61,128,32]{0,2,1:T(8,128)S(1)} fusion(f32[61,128,32]{0,2,1:T(8,128)S(1)} %broadcast_in_dim.21, s32[128]{0:T(128)S(1)} %fusion.4, f32[128,61,32]{1,2,0:T(8,128)} %bitcast.133), kind=kCustom, calls=%fused_computation.2 | custom fusion | bytes 2998784 | tf_op jit(solution)/shard_map/scatter | solution.py:111
  290.1 19.8 %psum.7 = f32[]{:T(128)} all-reduce(f32[]{:T(128)S(6)} %convert_element_type.47), channel_id=1, replica_groups=mesh['view'=4,'gauss'=8] {'gauss'}, use_global_device_ids=true, to_apply=%region_10.11 | all-reduce | flops 1 | bytes 8 | tf_op jit(solution)/shard_map/psum | solution.py:79
  311.3 9.7 %all-gather.3.cloned.1.call-done = f32[244,128,32]{1,2,0:T(8,128)} async-done(((f32[61,128,32]{1,2,0:T(8,128)}), f32[244,128,32]{1,2,0:T(8,128)}) %all-gather.3.cloned.1.call-update) | async-done | bytes 3997712 | tf_op jit(solution)/shard_map/all_gather | solution.py:113
  321.1 9.3 %copy.28 = f32[61,128,4,32]{0,3,2,1:T(8,128)} copy(f32[61,128,4,32]{1,3,0,2:T(8,128)} %bitcast.136) | data formatting | bytes 7995392 | tf_op jit(solution)/shard_map/reshape | solution.py:114
  330.3 6.8 %copy.29 = f32[61,16384]{1,0:T(8,128)} copy(f32[61,16384]{0,1:T(8,128)} %bitcast.131) | data formatting | bytes 7995392
  (77 shorter events, 47.7 us)
Async XLA Ops:
  7.2 65.9 %copy-start = (f32[3,16384]{1,0:T(4,128)S(1)}, f32[3,16384]{1,0:T(4,128)}, u32[]{:S(2)}) copy-start(f32[3,16384]{1,0:T(4,128)} %param.12) | copy-start | bytes 589828
  7.2 107.3 %copy-start.6 = (s32[4,16384]{1,0:T(4,128)S(1)}, s32[4,16384]{1,0:T(4,128)}, u32[]{:S(2)}) copy-start(s32[4,16384]{1,0:T(4,128)} %param.17) | copy-start | bytes 786436
  8.2 106.5 %copy-start.2 = (f32[3,16384]{1,0:T(4,128)S(1)}, f32[3,16384]{1,0:T(4,128)}, u32[]{:S(2)}) copy-start(f32[3,16384]{1,0:T(4,128)} %param.13) | copy-start | bytes 589828
  8.8 106.1 %copy-start.3 = (f32[4,2,16384]{2,1,0:T(2,128)S(1)}, f32[4,2,16384]{2,1,0:T(2,128)}, u32[]{:S(2)}) copy-start(f32[4,2,16384]{2,1,0:T(2,128)} %param.16) | copy-start | bytes 1572868
  35.2 202.2 %all-to-all-start = ((s32[1,8,16]{2,0,1:T(1,128)}), s32[1,8,16]{2,0,1:T(1,128)S(1)}, u32[]{:S(2)}, u32[]{:S(2)}) async-start(s32[1,8,16]{2,0,1:T(1,128)} %compare_select_fusion.1), calls=%async_computation | async-start | bytes 8192 | tf_op jit(solution)/shard_map/all_to_all | solution.py:105
  38.5 112.6 %all-reduce.4.cloned.1.call-start = ((), (), s32[]{:S(2)}) async-start(), calls=%async_computation.3 | async-start | bytes 262144 | tf_op jit(solution)/shard_map/pmax | solution.py:70
  79.3 71.8 %copy-start.1 = (f32[4,16384]{1,0:T(4,128)S(1)}, f32[4,16384]{1,0:T(4,128)}, u32[]{:S(2)}) copy-start(f32[4,16384]{1,0:T(4,128)} %param.14) | copy-start | bytes 786436
  237.4 29.4 %all-to-all-start.1 = ((f32[8,1,31232]{2,1,0:T(1,128)}), f32[8,1,31232]{2,1,0:T(1,128)S(1)}, u32[]{:S(2)}, u32[]{:S(2)}) async-start(f32[8,1,31232]{2,1,0:T(1,128)} %reshape.633), calls=%async_computation.1 | async-start | bytes 1998848 | tf_op jit(solution)/shard_map/all_to_all | solution.py:104
  242.9 78.2 %all-gather.3.cloned.1.call-start = ((), (), s32[]{:S(2)}) async-start(), calls=%async_computation.2 | async-start | bytes 4997120 | tf_op jit(solution)/shard_map/all_gather | solution.py:113
  274.9 35.6 %copy-start.4 = (f32[1,16384]{1,0:T(1,128)S(1)}, f32[1,16384]{1,0:T(1,128)}, u32[]{:S(2)}) copy-start(f32[1,16384]{1,0:T(1,128)} %get-tuple-element.97) | copy-start | bytes 196612
  274.9 35.6 %copy-start.5 = (f32[1,16384]{1,0:T(1,128)S(1)}, f32[1,16384]{1,0:T(1,128)}, u32[]{:S(2)}) copy-start(f32[1,16384]{1,0:T(1,128)} %get-tuple-element.98) | copy-start | bytes 196612
Sparse Core Ops, SparseCore 0:
  117.9 33.1 all-reduce.3
  289.6 31.4 all-gather.2
